TPU v7x, 256 devices: a whole 4x4x8 slice. The times are simulated.
256 devices in a mesh: lat: 16 (over z, y_hi), lon: 16 (over x, y_lo, core).
Axes of the slice: x: 4, y: 4 (y_hi: 2, y_lo: 2; y = y_hi * 2 + y_lo), z: 8, core: 2. Of those that a mesh axis runs over, the one named last changes fastest.
Arguments:
- x_fwd: bfloat16 [256, 1536, 256], P('lat', 'lon'), may hold values from -6 to 6
- x_prev: bfloat16 [256, 1536, 256], P('lat', 'lon'), may hold values from -6 to 6
- grad_out: bfloat16 [256, 1536, 256], P('lat', 'lon'), may hold values from -6 to 6
- weight: bfloat16 [2048, 256], replicated, may hold values from -0.125 to 0.125
- basis: bfloat16 [256, 8, 3, 49], P('lat'), may hold values from -1.5 to 1.5
- lon_reach: int32 [256], P('lat'), may hold values from 1 to 24, as said below
- lat_reach: int32 [256], P('lat'), may hold values from 0 to 1, as said below
Outputs:
- output: bfloat16 [256, 1536, 256], P('lat', 'lon')
- grad_in: bfloat16 [256, 1536, 256], P('lat', 'lon')
- grad_weight: float32 [2048, 256], P(('lat', 'lon'))
Inputs may be any that keep to these rules, and one draw needn't show every extreme that they name: `lon_reach`: reaches widen toward the two poles; the cycles nearest the poles reach 24. `lat_reach`: the first and the last cycle of every aligned block of 16 cycles reach 1.
All inputs are finite; a program needn't handle non-finite values.
Results may differ from a plain program's by a relative error of at most 0.0049.
Values may be sent and summed in bfloat16 or wider, within the bound.
No kernel may reach another device: no remote copies, remote signals or barrier semaphores. Data moves between devices by JAX's collectives and lax.ppermute only.
A program may use at most 192 MiB of HBM per device.

v0:
```python
import jax
import jax.numpy as jnp
from jax import lax
from jax.sharding import PartitionSpec as P


def padded_2(block, sides, width, periodic):
    for axis, dim in sides:
        count = lax.axis_size(axis)
        forward = [(i, i + 1) for i in range(count - 1)]
        if periodic:
            forward.append((count - 1, 0))
        backward = [(target, source) for source, target in forward]
        low = lax.ppermute(
            lax.slice_in_dim(block, block.shape[dim] - width, None, axis=dim), axis, forward
        )
        high = lax.ppermute(lax.slice_in_dim(block, 0, width, axis=dim), axis, backward)
        block = jnp.concatenate([low, block, high], axis=dim)
    return block


def passed_along(value, axis, steps):
    count = lax.axis_size(axis)
    pairs = [(source, (source + steps) % count) for source in range(count)]
    return lax.ppermute(value, axis, pairs)


def shifted(value, axis, steps):
    count = lax.axis_size(axis)
    leading, last = (max(0, -steps), min(count, count - steps))
    return lax.ppermute(value, axis, [(source, source + steps) for source in range(leading, last)])


def local(x_fwd, x_prev, grad_out, weight, basis, lon_reach, lat_reach):
    row_count, col_count, chan_count = x_fwd.shape
    basis_count = basis.shape[1]
    tap_count = basis.shape[3]
    cycle_reach = (tap_count - 1) // 2
    pad_width = col_count + 2 * cycle_reach
    lat_taps = jnp.arange(3, dtype=jnp.int32)
    lon_taps = jnp.arange(tap_count, dtype=jnp.int32)
    live_taps = (jnp.abs(lat_taps - 1)[None, :, None] <= lat_reach[:, None, None]) & (
        jnp.abs(lon_taps - cycle_reach)[None, None, :] <= lon_reach[:, None, None]
    )
    filters = jnp.where(live_taps[:, None, :, :], basis, jnp.zeros_like(basis))
    offsets = (
        jnp.arange(pad_width, dtype=jnp.int32)[:, None]
        - jnp.arange(col_count, dtype=jnp.int32)[None, :]
    )
    tap_select = (offsets[:, :, None] == lon_taps[None, None, :]).astype(jnp.bfloat16)
    toeplitz = jnp.einsum(
        "rkab,pob->rakpo", filters, tap_select, preferred_element_type=jnp.float32
    ).astype(jnp.bfloat16)
    stacked = jnp.stack([x_fwd, x_prev], axis=0)
    tall_block = padded_2(stacked, (("lat", 1),), 1, False)
    padded = padded_2(tall_block, (("lon", 2),), cycle_reach, True)

    def basis_conv(source):
        window = jnp.stack(
            [source[shift_row : shift_row + row_count] for shift_row in range(3)], axis=1
        )
        conv = jnp.einsum("rakpo,rapc->rokc", toeplitz, window, preferred_element_type=jnp.float32)
        return conv.astype(jnp.bfloat16).reshape(row_count * col_count, basis_count * chan_count)

    conv_fwd = basis_conv(padded[0])
    output = (
        jnp.dot(conv_fwd, weight, preferred_element_type=jnp.float32)
        .astype(jnp.bfloat16)
        .reshape(row_count, col_count, chan_count)
    )
    conv_prev = basis_conv(padded[1])
    grad_flat = grad_out.reshape(row_count * col_count, chan_count)
    grad_conv = lax.dot_general(
        grad_flat, weight, (((1,), (1,)), ((), ())), preferred_element_type=jnp.float32
    ).astype(jnp.bfloat16)
    grad_conv = grad_conv.reshape(row_count, col_count, basis_count, chan_count)
    contributions = jnp.einsum(
        "rakpo,rokc->rapc", toeplitz, grad_conv, preferred_element_type=jnp.float32
    )
    spread_grad = jnp.pad(contributions[:, 0], ((0, 2), (0, 0), (0, 0)))
    spread_grad = spread_grad + jnp.pad(contributions[:, 1], ((1, 1), (0, 0), (0, 0)))
    spread_grad = spread_grad + jnp.pad(contributions[:, 2], ((2, 0), (0, 0), (0, 0)))
    left_rim = spread_grad[:, :cycle_reach]
    right_rim = spread_grad[:, cycle_reach + col_count :]
    core_cols = spread_grad[:, cycle_reach : cycle_reach + col_count]
    from_right = passed_along(left_rim.astype(jnp.bfloat16), "lon", -1).astype(left_rim.dtype)
    from_left = passed_along(right_rim.astype(jnp.bfloat16), "lon", 1).astype(right_rim.dtype)
    filler = jnp.zeros((row_count + 2, col_count - 2 * cycle_reach, chan_count), jnp.float32)
    core_cols = core_cols + jnp.concatenate([from_left, filler, from_right], axis=1)
    from_below = shifted(core_cols[0], "lat", -1)
    from_above = shifted(core_cols[row_count + 1].astype(jnp.bfloat16), "lat", 1).astype(
        jnp.float32
    )
    inner_rows = core_cols[1 : row_count + 1]
    inner_rows = inner_rows.at[0].add(from_above).at[row_count - 1].add(from_below)
    grad_in = inner_rows.astype(jnp.bfloat16)
    share_rows = weight.shape[0] // lax.axis_size(("lat", "lon"))
    partial_value = lax.dot_general(
        conv_prev, grad_flat, (((0,), (0,)), ((), ())), preferred_element_type=jnp.float32
    )
    summed = lax.psum(partial_value, ("lat", "lon"))
    first_row = lax.axis_index(("lat", "lon")) * share_rows
    grad_weight = lax.dynamic_slice_in_dim(summed, first_row, share_rows, 0)
    return (output, grad_in, grad_weight)


def solution(mesh):
    return jax.shard_map(
        local,
        mesh=mesh,
        in_specs=(
            P("lat", "lon", None),
            P("lat", "lon", None),
            P("lat", "lon", None),
            P(),
            P("lat", None, None, None),
            P("lat"),
            P("lat"),
        ),
        out_specs=(P("lat", "lon", None), P("lat", "lon", None), P(("lat", "lon"), None)),
        check_vma=False,
    )
```

profile of v0, /device:TPU:2, one launch (start us, length us, event | category | flops | bytes accessed | tf_op | source)
XLA Modules:
  0.0 430.2 jit_solution(15524919795056145211)
XLA Ops:
  8.4 3.0 convolution_convert_fusion
  11.4 5.4 %copy.48 = bf16[192,8,8,256]{3,2,1,0:T(8,128)(2,1)} copy(bf16[192,8,8,256]{3,1,2,0:T(8,128)(2,1)S(1)} %bitcast.108) | data formatting | bytes 12582912
  17.1 7.1 %convert_bitcast_fusion = bf16[16,3,8,144,96]{4,0,1,2,3:T(8,128)(2,1)} fusion(s32[144,96]{1,0:T(8,128)S(1)} %iota_subtract_fusion, bf16[16,8,3,49]{3,1,2,0:T(8,128)(2,1)S(1)} %broadcast_select_fusion), kind=kOutput, calls=%fused_computation | convolution fusion | flops 526210560 | bytes 10709760 | tf_op jit(solution)/shard_map/rkab,pob->rakpo/dot_general | solution.py:51
  24.2 38.1 %copy.35 = bf16[16,3,8,144,96]{3,2,4,1,0:T(8,128)(2,1)} copy(bf16[16,3,8,144,96]{4,0,1,2,3:T(8,128)(2,1)} %convert_bitcast_fusion) | data formatting | bytes 21233664 | tf_op jit(solution)/shard_map/convert_element_type | solution.py:53
  62.3 12.7 %fusion.20 = f32[16,3,144,256]{3,2,1,0:T(8,128)} fusion(bf16[16,3,8,144,96]{3,2,4,1,0:T(8,128)(2,1)} %copy.35, bf16[16,96,8,256]{3,2,1,0:T(8,128)(2,1)} %bitcast.117), kind=kOutput, calls=%fused_computation.21 | convolution fusion | flops 2717908992 | bytes 23986176 | tf_op jit(solution)/shard_map/rakpo,rokc->rapc/dot_general | solution.py:77
  75.0 3.6 slice_bitcast_fusion.2
  79.4 2.6 collective-permute-start.5
  82.1 5.1 %collective-permute-start = (bf16[2,1,96,256]{3,2,1,0:T(8,128)(2,1)S(1)}, bf16[2,1,96,256]{3,2,1,0:T(8,128)(2,1)S(1)}, u32[]{:S(2)}, u32[]{:S(2)}) collective-permute-start(bf16[2,1,96,256]{3,2,1,0:T(8,128)(2,1)S(1)} %get-tuple-element.42), channel_id=1, source_target_pairs={{0,16},{16,32},{32,48},{48,64},{64,80},{80,96},{96,112},{112,128},... | collective-permute-start | bytes 294920 | tf_op jit(solution)/shard_map/ppermute | solution.py:14
  89.0 6.1 %collective-permute-start.6 = (bf16[96,256]{1,0:T(8,128)(2,1)S(1)}, bf16[96,256]{1,0:T(8,128)(2,1)S(1)}, u32[]{:S(2)}, u32[]{:S(2)}) collective-permute-start(bf16[96,256]{1,0:T(8,128)(2,1)S(1)} %fusion.26), channel_id=1, source_target_pairs={{0,16},{16,32},{32,48},{48,64},{64,80},{80,96},{96,112},{112,128},... | collective-permute-start | bytes 147464 | tf_op jit(solution)/shard_map/ppermute | solution.py:31
  96.0 2.8 collective-permute-start.3
  102.2 8.8 %collective-permute-done.7 = f32[96,256]{1,0:T(8,128)} collective-permute-done((f32[96,256]{1,0:T(8,128)}, f32[96,256]{1,0:T(8,128)}, u32[]{:S(2)}, u32[]{:S(2)}) %collective-permute-start.7) | collective-permute-done | bytes 98336 | tf_op jit(solution)/shard_map/ppermute | solution.py:31
  111.0 1.6 fusion.22
  112.6 2.4 convert_element_type.56
  115.0 1.4 pad_maximum_fusion
  116.5 3.1 slice_bitcast_fusion.5
  119.5 25.3 %fusion.5 = bf16[16,96,8,256]{3,1,2,0:T(8,128)(2,1)S(1)} fusion(bf16[16,3,8,144,96]{4,0,1,2,3:T(8,128)(2,1)} %convert_bitcast_fusion, bf16[16,1,144,256]{3,2,0,1:T(8,128)(2,1)} %get-tuple-element.33, bf16[16,1,144,256]{3,2,0,1:T(8,128)(2,1)} %get-tuple-element.34, bf16[16,1,144,256]{3,2,0,1:T(8,128)(2,1)} %get-tuple-element.32), kind=kOutput, calls=%fused_computation.9 | convolution fusion | flops 2724593664 | bytes 20447232 | tf_op jit(solution)/shard_map/rakpo,rapc->rokc/dot_general | solution.py:62
  144.8 4.4 %copy.31 = bf16[16,96,8,256]{3,2,1,0:T(8,128)(2,1)S(1)} copy(bf16[16,96,8,256]{3,1,2,0:T(8,128)(2,1)S(1)} %fusion.5) | data formatting | bytes 12582912 | tf_op jit(solution)/shard_map/convert_element_type | solution.py:63
  149.2 2.8 copy.49
  152.0 3.4 fusion.30
  155.4 26.2 %fusion.4 = bf16[16,96,8,256]{3,1,2,0:T(8,128)(2,1)} fusion(bf16[16,3,8,144,96]{4,0,1,2,3:T(8,128)(2,1)} %convert_bitcast_fusion, bf16[16,1,144,256]{3,2,1,0:T(8,128)(2,1)S(1)} %copy-done.5, bf16[16,1,144,256]{3,2,1,0:T(8,128)(2,1)S(1)} %copy-done.6, bf16[16,1,144,256]{3,2,1,0:T(8,128)(2,1)} %get-tuple-element.37), kind=kOutput, calls=%fused_computation.8 | convolution fusion | flops 2731671552 | bytes 20447232 | tf_op jit(solution)/shard_map/rakpo,rapc->rokc/dot_general | solution.py:62
  181.6 7.1 %copy.24 = bf16[16,96,8,256]{3,2,1,0:T(8,128)(2,1)S(1)} copy(bf16[16,96,8,256]{3,1,2,0:T(8,128)(2,1)} %fusion.4) | data formatting | bytes 12582912 | tf_op jit(solution)/shard_map/convert_element_type | solution.py:63
  188.7 2.7 copy.47
  191.5 2.8 convolution_convert_fusion.1
  194.2 227.6 %all-reduce.5.cloned.1.call-done = f32[2048,256]{1,0:T(8,128)} async-done(((f32[2048,256]{1,0:T(8,128)}), f32[2048,256]{1,0:T(8,128)}) %all-reduce.5.cloned.1.call-update) | async-done | bytes 2097168 | tf_op jit(solution)/shard_map/psum | solution.py:101
  (61 shorter events, 9.6 us)
Async XLA Ops:
  7.2 1.2 copy-start
  7.2 414.6 %all-reduce.5.cloned.1.call-start = ((), (), s32[]{:S(2)}) async-start(), calls=%async_computation | async-start | bytes 4194304 | tf_op jit(solution)/shard_map/psum | solution.py:101
  11.4 5.4 %copy-start.12 = (s32[16]{0:T(128)S(1)}, s32[16]{0:T(128)}, u32[]{:S(2)}) copy-start(s32[16]{0:T(128)} %param.16) | copy-start | bytes 196
  11.4 5.5 %copy-start.13 = (s32[16]{0:T(128)S(1)}, s32[16]{0:T(128)}, u32[]{:S(2)}) copy-start(s32[16]{0:T(128)} %param.17) | copy-start | bytes 196
  11.4 5.6 %copy-start.11 = (bf16[16,8,3,49]{3,1,2,0:T(8,128)(2,1)S(1)}, bf16[16,8,3,49]{3,1,2,0:T(8,128)(2,1)}, u32[]{:S(2)}) copy-start(bf16[16,8,3,49]{3,1,2,0:T(8,128)(2,1)} %param.15) | copy-start | bytes 112900
  78.6 3.5 copy-start.1
  78.6 3.5 copy-start.2
  79.3 9.2 %collective-permute-start.4 = (bf16[18,24,256]{2,1,0:T(8,128)(2,1)S(1)}, bf16[18,24,256]{2,1,0:T(8,128)(2,1)S(1)}, u32[]{:S(2)}, u32[]{:S(2)}) collective-permute-start(bf16[18,24,256]{2,1,0:T(8,128)(2,1)S(1)} %get-tuple-element.44), channel_id=1, source_target_pairs={{0,1},{1,2},{2,3},{3,4},{4,5},{5,6},{6,7},{7,8},{8,9},{9,10},{10,1... | collective-permute-start | bytes 663560 | tf_op jit(solution)/shard_map/ppermute | solution.py:25
  79.4 9.2 %collective-permute-start.5 = (bf16[18,24,256]{2,1,0:T(8,128)(2,1)S(1)}, bf16[18,24,256]{2,1,0:T(8,128)(2,1)S(1)}, u32[]{:S(2)}, u32[]{:S(2)}) collective-permute-start(bf16[18,24,256]{2,1,0:T(8,128)(2,1)S(1)} %get-tuple-element.45), channel_id=1, source_target_pairs={{0,15},{1,0},{2,1},{3,2},{4,3},{5,4},{6,5},{7,6},{8,7},{9,8},{10,9... | collective-permute-start | bytes 663560 | tf_op jit(solution)/shard_map/ppermute | solution.py:25
  82.1 12.9 %collective-permute-start = (bf16[2,1,96,256]{3,2,1,0:T(8,128)(2,1)S(1)}, bf16[2,1,96,256]{3,2,1,0:T(8,128)(2,1)S(1)}, u32[]{:S(2)}, u32[]{:S(2)}) collective-permute-start(bf16[2,1,96,256]{3,2,1,0:T(8,128)(2,1)S(1)} %get-tuple-element.42), channel_id=1, source_target_pairs={{0,16},{16,32},{32,48},{48,64},{64,80},{80,96},{96,112},{112,128},... | collective-permute-start | bytes 294920 | tf_op jit(solution)/shard_map/ppermute | solution.py:14
  87.2 8.0 %collective-permute-start.1 = (bf16[2,1,96,256]{3,2,1,0:T(8,128)(2,1)S(1)}, bf16[2,1,96,256]{3,2,1,0:T(8,128)(2,1)S(1)}, u32[]{:S(2)}, u32[]{:S(2)}) collective-permute-start(bf16[2,1,96,256]{3,2,1,0:T(8,128)(2,1)S(1)} %get-tuple-element.43), channel_id=1, source_target_pairs={{16,0},{32,16},{48,32},{64,48},{80,64},{96,80},{112,96},{128,112},... | collective-permute-start | bytes 294920 | tf_op jit(solution)/shard_map/ppermute | solution.py:17
  89.0 10.1 %collective-permute-start.6 = (bf16[96,256]{1,0:T(8,128)(2,1)S(1)}, bf16[96,256]{1,0:T(8,128)(2,1)S(1)}, u32[]{:S(2)}, u32[]{:S(2)}) collective-permute-start(bf16[96,256]{1,0:T(8,128)(2,1)S(1)} %fusion.26), channel_id=1, source_target_pairs={{0,16},{16,32},{32,48},{48,64},{64,80},{80,96},{96,112},{112,128},... | collective-permute-start | bytes 147464 | tf_op jit(solution)/shard_map/ppermute | solution.py:31
  95.0 1.0 copy-start.7
  95.2 0.8 copy-start.9
  96.0 19.0 %collective-permute-start.2 = (bf16[2,18,24,256]{3,2,1,0:T(8,128)(2,1)}, bf16[2,18,24,256]{3,2,1,0:T(8,128)(2,1)S(1)}, u32[]{:S(2)}, u32[]{:S(2)}) collective-permute-start(bf16[2,18,24,256]{3,2,1,0:T(8,128)(2,1)} %get-tuple-element.40), channel_id=1, source_target_pairs={{0,1},{1,2},{2,3},{3,4},{4,5},{5,6},{6,7},{7,8},{8,9},{9,10},{10,1... | collective-permute-start | bytes 1327112 | tf_op jit(solution)/shard_map/ppermute | solution.py:14
  96.0 19.0 %collective-permute-start.3 = (bf16[2,18,24,256]{3,2,1,0:T(8,128)(2,1)S(1)}, bf16[2,18,24,256]{3,2,1,0:T(8,128)(2,1)}, u32[]{:S(2)}, u32[]{:S(2)}) collective-permute-start(bf16[2,18,24,256]{3,2,1,0:T(8,128)(2,1)S(1)} %get-tuple-element.41), channel_id=1, source_target_pairs={{1,0},{2,1},{3,2},{4,3},{5,4},{6,5},{7,6},{8,7},{9,8},{10,9},{11,1... | collective-permute-start | bytes 1327112 | tf_op jit(solution)/shard_map/ppermute | solution.py:17
  99.7 1.2 copy-start.3
  100.9 10.1 %collective-permute-start.7 = (f32[96,256]{1,0:T(8,128)}, f32[96,256]{1,0:T(8,128)}, u32[]{:S(2)}, u32[]{:S(2)}) collective-permute-start(f32[96,256]{1,0:T(8,128)} %get-tuple-element.38), channel_id=1, source_target_pairs={{16,0},{32,16},{48,32},{64,48},{80,64},{96,80},{112,96},{128,112},... | collective-permute-start | bytes 294920 | tf_op jit(solution)/shard_map/ppermute | solution.py:31
  102.2 12.8 %copy-start.8 = (bf16[2,1,96,256]{3,2,1,0:T(8,128)(2,1)S(1)}, bf16[2,1,96,256]{3,2,1,0:T(8,128)(2,1)}, u32[]{:S(2)}) copy-start(bf16[2,1,96,256]{3,2,1,0:T(8,128)(2,1)} %copy-done.7) | copy-start | bytes 294916
  102.2 12.8 %copy-start.10 = (bf16[2,1,96,256]{3,2,1,0:T(8,128)(2,1)S(1)}, bf16[2,1,96,256]{3,2,1,0:T(8,128)(2,1)}, u32[]{:S(2)}) copy-start(bf16[2,1,96,256]{3,2,1,0:T(8,128)(2,1)} %copy-done.9) | copy-start | bytes 294916
  149.2 2.8 copy-start.4
  152.0 3.4 copy-start.5
  152.0 3.4 copy-start.6
Sparse Core Ops, SparseCore 0:
  155.5 266.2 all-reduce.4
where the time goes:
time: 435 us; the launch traced here: 430 us
  waiting for transfers between devices  237 us (54%)
  matrix products  80.4 us (18%)
  local copies, waits for them, and re-layouts  71 us (16%)
  starting transfers between devices  19.3 us (4%)
  between operations  14.6 us (3%)
  other arithmetic  8.2 us (2%)
    psum x1, waiting for transfers between devices, local(): summed = lax.psum(partial_value, ('lat', 'lon'))  228 us
    dot_general x2, matrix products, basis_conv(): jnp.einsum('rakpo,rapc->rokc', toeplitz, window, preferred_element_type=j...  51.5 us
    convert_element_type x1, local copies, waits for them, and re-layouts, local(): toeplitz = jnp.einsum('rkab,pob->rakpo', filters, tap_select, preferred_e...  38.1 us
    unnamed x31, local copies, waits for them, and re-layouts  13.2 us
    dot_general x1, matrix products, local(): jnp.einsum('rakpo,rokc->rapc', toeplitz, grad_conv, preferred_element_typ...  12.7 us
    convert_element_type x2, local copies, waits for them, and re-layouts, basis_conv(): conv.astype(jnp.bfloat16)  11.4 us
    ppermute x2, waiting for transfers between devices, shifted(): lax.ppermute(value, axis, [(source, source + steps) for source in range(l...  8.83 us
  transfers between devices with their start and end apart: 9, of which 3 were waited for; matrix products, arithmetic and copies ran while one was open for 10% of the time, Pallas kernels for 0%

commit v1 on v0

v1 whole, which is shorter than its diff:
```python
import jax
import jax.numpy as jnp
from jax import lax
from jax.experimental import pallas as pl
from jax.experimental.pallas import tpu as pltpu
from jax.sharding import PartitionSpec as P


F32 = jnp.float32
BF16 = jnp.bfloat16
REACH = 24
GROUP = 32
SPAN = 80
LANES = 256
CONV_UNROLL = 16
GRAD_UNROLL = 8


def dot(lhs, rhs, dims):
    return lax.dot_general(lhs, rhs, (dims, ((), ())), preferred_element_type=F32)


def params():
    return pltpu.CompilerParams(vmem_limit_bytes=56 * 1024 * 1024)


def vmem(count):
    return [pl.BlockSpec(memory_space=pltpu.VMEM)] * count


def banded(taps):
    pieces = []
    for k in range(taps.shape[0]):
        wide = jnp.broadcast_to(taps[k : k + 1], (GROUP, LANES))
        pieces.append(pltpu.roll(wide, 0, 1, stride=1, stride_axis=0).astype(BF16))
    return jnp.concatenate(pieces, axis=0)


def grads_kernel(
    flat_ref, grad_ref, north_ref, south_ref, weight_ref, x_ref, bands_ref, core_ref, to_east_ref, to_west_ref, gc_ref, spread_ref
):
    rows, cols, chans = grad_ref.shape
    basis = flat_ref.shape[1]
    cells = rows * cols
    spread_ref[...] = jnp.zeros(spread_ref.shape, F32)
    grads = grad_ref[...].reshape(cells, chans)
    outer = jnp.concatenate([north_ref[2 * cols : 3 * cols, :], south_ref[2 * cols : 3 * cols, :]], axis=0)
    for k in range(basis):
        mix = weight_ref[k * chans : (k + 1) * chans, :]
        gc_ref[:cells, k * chans : (k + 1) * chans] = dot(grads, mix, (((1,), (1,)))).astype(BF16)
        gc_ref[cells:, k * chans : (k + 1) * chans] = dot(outer, mix, (((1,), (1,)))).astype(BF16)

    def spread_row(band, line, row, lat_taps):
        for g in range(cols // GROUP):
            first = line * cols + g * GROUP
            cell = jnp.concatenate(
                [gc_ref[pl.ds(first, GROUP), k * chans : (k + 1) * chans] for k in range(basis)], axis=0
            )
            part = dot(band, cell, (((0,), (0,))))
            for a in lat_taps:
                spread_ref[row + a, g * GROUP : g * GROUP + SPAN, :] += part[a * SPAN : (a + 1) * SPAN]

    def one_row(r, carry):
        band = banded(flat_ref[r].astype(F32))
        bands_ref[r] = band
        spread_row(band, r, r, range(3))
        return carry

    lax.fori_loop(0, rows, one_row, 0, unroll=GRAD_UNROLL)
    spread_row(banded(north_ref[3 * cols :, :].astype(F32)), rows, -1, (2,))
    spread_row(banded(south_ref[3 * cols :, :].astype(F32)), rows + 1, rows, (0,))
    core_ref[...] = spread_ref[1 : rows + 1, REACH : REACH + cols, :]
    tall = rows + 2
    for low, at, send_ref in ((0, 0, to_west_ref), (REACH + cols, cols - REACH, to_east_ref)):
        send_ref[tall:] = spread_ref[1 : rows + 1, low : low + REACH, :].astype(BF16)
        send_ref[1 : rows + 1] = x_ref[:, at : at + REACH, :]
        send_ref[0] = north_ref[cols + at : cols + at + REACH, :]
        send_ref[rows + 1] = south_ref[cols + at : cols + at + REACH, :]


def fill_padded(x_ref, north_ref, south_ref, place, west_ref, east_ref, padded_ref):
    rows, cols, chans = x_ref.shape
    padded_ref[:, 2 * REACH + cols - 16 :, :] = jnp.zeros((rows + 2, 32, chans), BF16)
    padded_ref[:, :REACH, :] = west_ref[: rows + 2]
    padded_ref[1 : rows + 1, REACH : REACH + cols, :] = x_ref[...]
    padded_ref[0, REACH : REACH + cols, :] = north_ref[place * cols : (place + 1) * cols, :]
    padded_ref[rows + 1, REACH : REACH + cols, :] = south_ref[place * cols : (place + 1) * cols, :]
    padded_ref[:, REACH + cols : 2 * REACH + cols, :] = east_ref[: rows + 2]


def convolve(bands_ref, padded_ref, conv_ref, rows, cols, chans):
    def one_row(r, carry):
        band = bands_ref[r]
        for g in range(cols // GROUP):
            low = g * GROUP
            window = jnp.concatenate(
                [
                    padded_ref[r, low : low + SPAN, :],
                    padded_ref[r + 1, low : low + SPAN, :],
                    padded_ref[r + 2, low : low + SPAN + 16, :],
                ],
                axis=0,
            )
            conv = dot(band, window, (((1,), (0,)))).astype(BF16)
            for k in range(band.shape[0] // GROUP):
                conv_ref[pl.ds(r * cols + low, GROUP), k * chans : (k + 1) * chans] = conv[
                    k * GROUP : (k + 1) * GROUP
                ]
        return carry

    lax.fori_loop(0, rows, one_row, 0, unroll=CONV_UNROLL)


def weight_kernel(
    core_ref, bands_ref, x_ref, north_ref, south_ref, west_ref, east_ref, grad_ref, keep_ref, send_ref, padded_ref, conv_ref
):
    rows, cols, chans = x_ref.shape
    fill_padded(x_ref, north_ref, south_ref, 0, west_ref, east_ref, padded_ref)
    convolve(bands_ref, padded_ref, conv_ref, rows, cols, chans)
    grads = grad_ref[...].reshape(rows * cols, chans)
    first = core_ref[0] == 0
    half = chans // 2
    for k in range(conv_ref.shape[1] // chans):
        part = dot(conv_ref[:, k * chans : (k + 1) * chans], grads, (((0,), (0,))))
        part = part.reshape(chans // 16, 2, 8, chans)
        even, odd = (part[:, 0].reshape(half, chans), part[:, 1].reshape(half, chans))
        keep_ref[k * half : (k + 1) * half, :] = jnp.where(first, even, odd)
        send_ref[k * half : (k + 1) * half, :] = jnp.where(first, odd, even).astype(BF16)


def forward_kernel(bands_ref, x_ref, north_ref, south_ref, west_ref, east_ref, weight_ref, out_ref, padded_ref, conv_ref):
    rows, cols, chans = x_ref.shape
    fill_padded(x_ref, north_ref, south_ref, 1, west_ref, east_ref, padded_ref)
    convolve(bands_ref, padded_ref, conv_ref, rows, cols, chans)
    step = 4
    for r in range(0, rows, step):
        out_ref[r : r + step] = (
            dot(conv_ref[r * cols : (r + step) * cols, :], weight_ref[...], (((1,), (0,))))
            .astype(BF16)
            .reshape(step, cols, chans)
        )


def finish_kernel(core_ref, west_ref, east_ref, out_ref):
    rows, cols, _ = out_ref.shape
    tall = rows + 2
    out_ref[:, REACH : cols - REACH, :] = core_ref[:, REACH : cols - REACH, :].astype(BF16)
    out_ref[:, :REACH, :] = (core_ref[:, :REACH, :] + west_ref[tall:].astype(F32)).astype(BF16)
    out_ref[:, cols - REACH :, :] = (core_ref[:, cols - REACH :, :] + east_ref[tall:].astype(F32)).astype(BF16)


def sent(value, axis, steps, periodic):
    count = lax.axis_size(axis)
    pairs = [(i, (i + steps) % count) for i in range(count) if periodic or 0 <= i + steps < count]
    return lax.ppermute(value, axis, pairs)


def bit_of(axis_bits):
    axis, bit = axis_bits
    return (lax.axis_index(axis) >> (bit.bit_length() - 1)) & 1


def exchanged(value, bits, flips):
    lat, lon = (lax.axis_size("lat"), lax.axis_size("lon"))
    lat_flip = sum(b for (axis, b), f in zip(bits, flips) if f and axis == "lat")
    lon_flip = sum(b for (axis, b), f in zip(bits, flips) if f and axis == "lon")
    pairs = []
    for i in range(lat):
        for j in range(lon):
            pairs.append((i * lon + j, (i ^ lat_flip) * lon + (j ^ lon_flip)))
    return lax.ppermute(value, ("lat", "lon"), pairs)


NAMES = (("lat", 8), ("lat", 4), ("lat", 2), ("lat", 1), ("lon", 8), ("lon", 4), ("lon", 2))


def stage(value, names, bits):
    dims = [names.index(b) for b in bits]
    own = [bit_of(b) for b in bits]

    def pick(flips):
        piece = value
        for dim, o, f in zip(dims, own, flips):
            piece = lax.dynamic_slice_in_dim(piece, o if not f else 1 - o, 1, dim)
        return jnp.squeeze(piece, tuple(dims))

    combos = [(1,)] if len(bits) == 1 else [(1, 1), (1, 0), (0, 1)]
    arrived = [exchanged(pick(flips).astype(BF16), bits, flips) for flips in combos]
    value = pick((0,) * len(bits))
    for piece in arrived:
        value = value + piece.astype(F32)
    return value, [n for n in names if n not in bits]


def scattered_sum(keep, send):
    names = list(NAMES)
    shape = (2,) * len(names) + (8, keep.shape[1])
    arrived = exchanged(send, (("lon", 1),), (1,))
    value = (keep + arrived.astype(F32)).reshape(shape)
    value, names = stage(value, names, (("lon", 2), ("lon", 4)))
    value, names = stage(value, names, (("lon", 8),))
    value = value.reshape((lax.axis_size("lat"),) + value.shape[-2:])
    return lax.all_to_all(value, "lat", 0, 0).sum(0)


def body(x_fwd, x_prev, grad_out, weight, basis, lon_reach, lat_reach):
    rows, cols, chans = x_fwd.shape
    basis_count = basis.shape[1]
    taps = basis.shape[3]
    cells = rows * cols
    wide = 2 * REACH + cols

    lane = jnp.arange(LANES, dtype=jnp.int32)
    live = (jnp.abs(lane // SPAN - 1)[None] <= lat_reach[:, None]) & (
        jnp.abs(lane % SPAN - REACH)[None] <= lon_reach[:, None]
    )
    flat = sum(
        jnp.pad(basis[:, :, a, :], ((0, 0), (0, 0), (a * SPAN, LANES - a * SPAN - taps))) for a in range(3)
    )
    flat = jnp.where(live[:, None, :], flat, jnp.zeros_like(flat))

    def line(r):
        return jnp.concatenate([x_prev[r], x_fwd[r], grad_out[r], flat[r]], axis=0)

    north = sent(line(rows - 1), "lat", 1, False)
    south = sent(line(0), "lat", -1, False)

    def tall_edge(field, low):
        edge = slice(low, low + REACH)
        return jnp.concatenate([north[None, edge], field[:, edge], south[None, edge]], axis=0)

    west_prev = sent(tall_edge(x_prev, cols - REACH), "lon", 1, True)
    east_prev = sent(tall_edge(x_prev, 0), "lon", -1, True)

    sides = jax.ShapeDtypeStruct((2 * rows + 2, REACH, chans), BF16)
    bands, core, to_east, to_west = pl.pallas_call(
        grads_kernel,
        out_shape=(
            jax.ShapeDtypeStruct((rows, basis_count * GROUP, LANES), BF16),
            jax.ShapeDtypeStruct((rows, cols, chans), F32),
            sides,
            sides,
        ),
        in_specs=vmem(6),
        out_specs=tuple(vmem(4)),
        scratch_shapes=[
            pltpu.VMEM((cells + 2 * cols, basis_count * chans), BF16),
            pltpu.VMEM((rows + 2, wide, chans), F32),
        ],
        compiler_params=params(),
        name="grads",
    )(flat, grad_out, north, south, weight, x_fwd)

    from_west = sent(to_east, "lon", 1, True)
    from_east = sent(to_west, "lon", -1, True)

    conv_scratch = [
        pltpu.VMEM((rows + 2, wide + 16, chans), BF16),
        pltpu.VMEM((cells, basis_count * chans), BF16),
    ]
    half = (weight.shape[0] // 2, chans)
    keep, send = pl.pallas_call(
        weight_kernel,
        out_shape=(jax.ShapeDtypeStruct(half, F32), jax.ShapeDtypeStruct(half, BF16)),
        in_specs=[pl.BlockSpec(memory_space=pltpu.SMEM)] + vmem(7),
        out_specs=tuple(vmem(2)),
        scratch_shapes=conv_scratch,
        compiler_params=params(),
        name="weight_grad",
    )(bit_of(("lon", 1)).reshape(1), bands, x_prev, north, south, west_prev, east_prev, grad_out)
    grad_weight = scattered_sum(keep, send)

    output = pl.pallas_call(
        forward_kernel,
        out_shape=jax.ShapeDtypeStruct(x_fwd.shape, BF16),
        in_specs=vmem(7),
        out_specs=vmem(1)[0],
        scratch_shapes=conv_scratch,
        compiler_params=params(),
        name="forward",
    )(bands, x_fwd, north, south, from_west, from_east, weight)

    grad_in = pl.pallas_call(
        finish_kernel,
        out_shape=jax.ShapeDtypeStruct(x_fwd.shape, BF16),
        in_specs=vmem(3),
        out_specs=vmem(1)[0],
        compiler_params=params(),
        name="finish",
    )(core, from_west, from_east)
    return (output, grad_in, grad_weight)


def solution(mesh):
    return jax.shard_map(
        body,
        mesh=mesh,
        in_specs=(
            P("lat", "lon", None),
            P("lat", "lon", None),
            P("lat", "lon", None),
            P(),
            P("lat", None, None, None),
            P("lat"),
            P("lat"),
        ),
        out_specs=(P("lat", "lon", None), P("lat", "lon", None), P(("lat", "lon"), None)),
        check_vma=False,
    )
```

time: 435 us -> 80.4 us (0.18)
  the two profiles are of different devices: /device:TPU:2 before, /device:TPU:16 now
where the time goes in v1:
time: 80.4 us; the launch traced here: 79.9 us
  starting transfers between devices  32.1 us (40%)
  Pallas kernels  24.4 us (30%)
  waiting for transfers between devices  12.9 us (16%)
  local copies, waits for them, and re-layouts  5.97 us (7%)
  other arithmetic  3.71 us (5%)
    ppermute x6, starting transfers between devices, sent(): return lax.ppermute(value, axis, pairs)  15.2 us
    all_to_all x1, starting transfers between devices, scattered_sum(): return lax.all_to_all(value, 'lat', 0, 0).sum(0)  11.3 us
    pallas_call x1, Pallas kernels, body(): pl.pallas_call(grads_kernel, out_shape=(jax.ShapeDtypeStruct((rows, basis...  8.27 us
    ppermute x5, waiting for transfers between devices, exchanged(): return lax.ppermute(value, ('lat', 'lon'), pairs)  7.97 us
    pallas_call x1, Pallas kernels, body(): pl.pallas_call(weight_kernel, out_shape=(jax.ShapeDtypeStruct(half, F32),...  6.8 us
    pallas_call x1, Pallas kernels, body(): pl.pallas_call(forward_kernel, out_shape=jax.ShapeDtypeStruct(x_fwd.shape...  6.75 us
    ppermute x5, starting transfers between devices, exchanged(): return lax.ppermute(value, ('lat', 'lon'), pairs)  5.65 us
    ppermute x6, waiting for transfers between devices, sent(): return lax.ppermute(value, axis, pairs)  4.88 us
  transfers between devices with their start and end apart: 12, of which 7 were waited for; matrix products, arithmetic and copies ran while one was open for 2% of the time, Pallas kernels for 22%

profile of v1, /device:TPU:16, one launch (start us, length us, event | category | flops | bytes accessed | tf_op | source)
XLA Modules:
  0.0 79.9 jit_solution(3407378702193766753)
XLA Ops:
  0.6 0.8 %slice_bitcast_fusion.8 = (bf16[16,8,49]{2,1,0:T(8,128)(2,1)S(1)}, bf16[16,8,49]{2,1,0:T(8,128)(2,1)S(1)}, bf16[16,8,49]{2,1,0:T(8,128)(2,1)S(1)}) fusion(bf16[16,8,3,49]{3,1,2,0:T(8,128)(2,1)} %param.11), kind=kLoop, calls=%fused_computation.26 | loop fusion | bytes 75264 | tf_op jit(solution)/shard_map/squeeze | solution.py:218
  1.4 0.7 compare_and_fusion
  2.3 0.9 %slice_bitcast_fusion.2 = (bf16[96,256]{1,0:T(8,128)(2,1)S(1)}, bf16[96,256]{1,0:T(8,128)(2,1)S(1)}) fusion(bf16[16,96,256]{2,1,0:T(8,128)(2,1)} %x_ref.5), kind=kLoop, calls=%fused_computation.20 | loop fusion | bytes 196608 | tf_op jit(solution)/shard_map/squeeze | solution.py:223
  3.2 0.9 %slice_bitcast_fusion = (bf16[96,256]{1,0:T(8,128)(2,1)S(1)}, bf16[96,256]{1,0:T(8,128)(2,1)S(1)}, bf16[96,256]{1,0:T(8,128)(2,1)S(1)}, bf16[96,256]{1,0:T(8,128)(2,1)S(1)}) fusion(bf16[16,96,256]{2,1,0:T(8,128)(2,1)} %grad_ref.3, bf16[16,96,256]{2,1,0:T(8,128)(2,1)} %x_ref.4), kind=kLoop, calls=%fused_computation.18 | loop fusion | bytes 393216 | tf_op jit(solution)/shard_map/squeeze | solution.py:223
  4.1 3.6 %collective-permute-start = (bf16[296,256]{1,0:T(8,128)(2,1)S(1)}, bf16[296,256]{1,0:T(8,128)(2,1)S(1)}, u32[]{:S(2)}, u32[]{:S(2)}) collective-permute-start(bf16[296,256]{1,0:T(8,128)(2,1)S(1)} %pad_maximum_fusion.2), channel_id=1, source_target_pairs={{0,16},{16,32},{32,48},{48,64},{64,80},{80,96},{96,112},{112,128},... | collective-permute-start | bytes 454664 | tf_op jit(solution)/shard_map/ppermute | solution.py:155
  7.7 3.8 %collective-permute-start.1 = (bf16[296,256]{1,0:T(8,128)(2,1)S(1)}, bf16[296,256]{1,0:T(8,128)(2,1)S(1)}, u32[]{:S(2)}, u32[]{:S(2)}) collective-permute-start(bf16[296,256]{1,0:T(8,128)(2,1)S(1)} %pad_maximum_fusion.3), channel_id=1, source_target_pairs={{16,0},{32,16},{48,32},{64,48},{80,64},{96,80},{112,96},{128,112},... | collective-permute-start | bytes 454664 | tf_op jit(solution)/shard_map/ppermute | solution.py:155
  11.5 1.1 %fusion.12 = (bf16[16,24,256]{2,1,0:T(8,128)(2,1)S(1)}, bf16[16,24,256]{2,1,0:T(8,128)(2,1)S(1)}) fusion(bf16[16,96,256]{2,1,0:T(8,128)(2,1)} %x_ref.5), kind=kLoop, calls=%fused_computation.45 | loop fusion | bytes 786432 | tf_op jit(solution)/shard_map/slice | solution.py:230
  13.2 4.2 %collective-permute-done.1.south_ref = bf16[296,256]{1,0:T(8,128)(2,1)S(1)} collective-permute-done((bf16[296,256]{1,0:T(8,128)(2,1)S(1)}, bf16[296,256]{1,0:T(8,128)(2,1)S(1)}, u32[]{:S(2)}, u32[]{:S(2)}) %collective-permute-start.1) | collective-permute-done | bytes 151584 | tf_op jit(solution)/shard_map/ppermute | solution.py:155
  17.6 3.9 %collective-permute-start.5 = (bf16[18,24,256]{2,1,0:T(8,128)(2,1)S(1)}, bf16[18,24,256]{2,1,0:T(8,128)(2,1)S(1)}, u32[]{:S(2)}, u32[]{:S(2)}) collective-permute-start(bf16[18,24,256]{2,1,0:T(8,128)(2,1)S(1)} %pad_maximum_fusion.1), channel_id=1, source_target_pairs={{0,15},{1,0},{2,1},{3,2},{4,3},{5,4},{6,5},{7,6},{8,7},{9,8},{10,9... | collective-permute-start | bytes 663560 | tf_op jit(solution)/shard_map/ppermute | solution.py:155
  21.5 8.3 %grads.1 = (bf16[16,256,256]{2,1,0:T(8,128)(2,1)}, f32[16,96,256]{2,1,0:T(8,128)}, bf16[34,24,256]{2,1,0:T(8,128)(2,1)}, bf16[34,24,256]{2,1,0:T(8,128)(2,1)}) custom-call(bf16[16,8,256]{2,1,0:T(8,128)(2,1)} %copy-done.4, bf16[16,96,256]{2,1,0:T(8,128)(2,1)} %grad_ref.3, bf16[296,256]{1,0:T(8,128)(2,1)} %copy-done.2, bf16[296,256]{1,0:T(8,128)(2,1)} %copy-done.3, ...), custom_call_target="tpu_custom_call" | custom-call | tf_op jit(solution)/shard_map/grads/pallas_call | solution.py:236
  30.6 6.8 %weight_grad.1 = (f32[1024,256]{1,0:T(8,128)}, bf16[1024,256]{1,0:T(8,128)(2,1)}) custom-call(s32[1]{0:T(128)} %bitcast.11.core_ref, bf16[16,256,256]{2,1,0:T(8,128)(2,1)} %get-tuple-element.9.bands_ref, bf16[16,96,256]{2,1,0:T(8,128)(2,1)} %x_ref.5, bf16[296,256]{1,0:T(8,128)(2,1)} %copy-done.2, bf16[296,256]{1,0:T(8,128)(2,1)} %copy-done.3, ...), custom_call_target="tpu_custom_call" | custom-call | tf_op jit(solution)/shard_map/weight_grad/pallas_call | solution.py:262
  37.4 2.1 %collective-permute-done.6 = bf16[1024,256]{1,0:T(8,128)(2,1)S(1)} collective-permute-done((bf16[1024,256]{1,0:T(8,128)(2,1)}, bf16[1024,256]{1,0:T(8,128)(2,1)S(1)}, u32[]{:S(2)}, u32[]{:S(2)}) %collective-permute-start.6) | collective-permute-done | bytes 524320 | tf_op jit(solution)/shard_map/ppermute | solution.py:171
  39.5 1.4 %convert_add_fusion = f32[1024,256]{1,0:T(8,128)S(1)} fusion(f32[1024,256]{1,0:T(8,128)} %get-tuple-element.13, bf16[1024,256]{1,0:T(8,128)(2,1)S(1)} %collective-permute-done.6), kind=kLoop, calls=%fused_computation | loop fusion | flops 524288 | bytes 2621440 | tf_op jit(solution)/shard_map/add | solution.py:199
  41.0 1.1 %collective-permute-start.7 = (bf16[2,2,2,2,2,8,256]{6,5,4,3,2,1,0:T(8,128)(2,1)S(1)}, bf16[2,2,2,2,2,8,256]{6,5,4,3,2,1,0:T(8,128)(2,1)S(1)}, u32[]{:S(2)}, u32[]{:S(2)}) collective-permute-start(bf16[2,2,2,2,2,8,256]{6,5,4,3,2,1,0:T(8,128)(2,1)S(1)} %get-tuple-element.15), channel_id=1, source_target_pairs={{0,6},{1,7},{2,4},{3,5},{4,2},{5,3},{6,0},{7,1},{8,14},{9,15},{10,... | collective-permute-start | bytes 393224 | tf_op jit(solution)/shard_map/ppermute | solution.py:171
  42.6 2.0 %collective-permute-start.8 = (bf16[2,2,2,2,2,8,256]{6,5,4,3,2,1,0:T(8,128)(2,1)S(1)}, bf16[2,2,2,2,2,8,256]{6,5,4,3,2,1,0:T(8,128)(2,1)S(1)}, u32[]{:S(2)}, u32[]{:S(2)}) collective-permute-start(bf16[2,2,2,2,2,8,256]{6,5,4,3,2,1,0:T(8,128)(2,1)S(1)} %get-tuple-element.17), channel_id=1, source_target_pairs={{0,2},{1,3},{2,0},{3,1},{4,6},{5,7},{6,4},{7,5},{8,10},{9,11},{10,... | collective-permute-start | bytes 393224 | tf_op jit(solution)/shard_map/ppermute | solution.py:171
  44.5 3.8 %collective-permute-done.7 = bf16[2,2,2,2,2,8,256]{6,5,4,3,2,1,0:T(8,128)(2,1)S(1)} collective-permute-done((bf16[2,2,2,2,2,8,256]{6,5,4,3,2,1,0:T(8,128)(2,1)S(1)}, bf16[2,2,2,2,2,8,256]{6,5,4,3,2,1,0:T(8,128)(2,1)S(1)}, u32[]{:S(2)}, u32[]{:S(2)}) %collective-permute-start.7) | collective-permute-done | bytes 131104 | tf_op jit(solution)/shard_map/ppermute | solution.py:171
  48.9 1.4 %collective-permute-done.8 = bf16[2,2,2,2,2,8,256]{6,5,4,3,2,1,0:T(8,128)(2,1)S(1)} collective-permute-done((bf16[2,2,2,2,2,8,256]{6,5,4,3,2,1,0:T(8,128)(2,1)S(1)}, bf16[2,2,2,2,2,8,256]{6,5,4,3,2,1,0:T(8,128)(2,1)S(1)}, u32[]{:S(2)}, u32[]{:S(2)}) %collective-permute-start.8) | collective-permute-done | bytes 131104 | tf_op jit(solution)/shard_map/ppermute | solution.py:171
  50.4 2.1 %collective-permute-start.10 = (bf16[2,2,2,2,8,256]{5,4,3,2,1,0:T(8,128)(2,1)S(1)}, bf16[2,2,2,2,8,256]{5,4,3,2,1,0:T(8,128)(2,1)S(1)}, u32[]{:S(2)}, u32[]{:S(2)}) collective-permute-start(bf16[2,2,2,2,8,256]{5,4,3,2,1,0:T(8,128)(2,1)S(1)} %fusion.5), channel_id=1, source_target_pairs={{0,8},{1,9},{2,10},{3,11},{4,12},{5,13},{6,14},{7,15},{8,0},{9,1},... | collective-permute-start | bytes 196616 | tf_op jit(solution)/shard_map/ppermute | solution.py:171
  52.5 3.9 %collective-permute-start.3 = (bf16[34,24,256]{2,1,0:T(8,128)(2,1)S(1)}, bf16[34,24,256]{2,1,0:T(8,128)(2,1)S(1)}, u32[]{:S(2)}, u32[]{:S(2)}) collective-permute-start(bf16[34,24,256]{2,1,0:T(8,128)(2,1)S(1)} %copy-done.7), channel_id=1, source_target_pairs={{0,15},{1,0},{2,1},{3,2},{4,3},{5,4},{6,5},{7,6},{8,7},{9,8},{10,9... | collective-permute-start | bytes 1253384 | tf_op jit(solution)/shard_map/ppermute | solution.py:155
  57.1 11.3 %all-to-all-start = ((f32[16,8,256]{2,1,0:T(8,128)}), f32[16,8,256]{2,1,0:T(8,128)S(1)}, u32[]{:S(2)}, u32[]{:S(2)}) async-start(f32[16,8,256]{2,1,0:T(8,128)} %bitcast.23), calls=%async_computation | async-start | bytes 262144 | tf_op jit(solution)/shard_map/all_to_all | solution.py:203
  68.4 0.7 copy-done
  69.2 0.8 copy-done.1
  69.9 6.7 %forward.1 = bf16[16,96,256]{2,1,0:T(8,128)(2,1)} custom-call(bf16[16,256,256]{2,1,0:T(8,128)(2,1)} %get-tuple-element.9.bands_ref, bf16[16,96,256]{2,1,0:T(8,128)(2,1)} %x_ref.4, bf16[296,256]{1,0:T(8,128)(2,1)} %copy-done.2, bf16[296,256]{1,0:T(8,128)(2,1)} %copy-done.3, bf16[34,24,256]{2,1,0:T(8,128)(2,1)} %copy-done, bf16[34,24,256]{2,1,0:T(8,128)(2,1)} %copy-done.1, ...), custom_call_target="tpu_custom_call" | custom-call | tf_op jit(solution)/shard_map/forward/pallas_call | solution.py:273
  76.7 2.6 %finish.1 = bf16[16,96,256]{2,1,0:T(8,128)(2,1)} custom-call(f32[16,96,256]{2,1,0:T(8,128)} %get-tuple-element.12.core_ref, bf16[34,24,256]{2,1,0:T(8,128)(2,1)} %copy-done, bf16[34,24,256]{2,1,0:T(8,128)(2,1)} %copy-done.1), custom_call_target="tpu_custom_call" | custom-call | tf_op jit(solution)/shard_map/finish/pallas_call | solution.py:283
  (42 shorter events, 4.4 us)
Async XLA Ops:
  2.3 19.2 %copy-start.4 = (bf16[16,8,256]{2,1,0:T(8,128)(2,1)}, bf16[16,8,256]{2,1,0:T(8,128)(2,1)S(1)}, u32[]{:S(2)}) copy-start(bf16[16,8,256]{2,1,0:T(8,128)(2,1)S(1)} %add_select_fusion.flat_ref) | copy-start | bytes 196612
  4.1 9.1 %collective-permute-start = (bf16[296,256]{1,0:T(8,128)(2,1)S(1)}, bf16[296,256]{1,0:T(8,128)(2,1)S(1)}, u32[]{:S(2)}, u32[]{:S(2)}) collective-permute-start(bf16[296,256]{1,0:T(8,128)(2,1)S(1)} %pad_maximum_fusion.2), channel_id=1, source_target_pairs={{0,16},{16,32},{32,48},{48,64},{64,80},{80,96},{96,112},{112,128},... | collective-permute-start | bytes 454664 | tf_op jit(solution)/shard_map/ppermute | solution.py:155
  7.7 9.7 %collective-permute-start.1 = (bf16[296,256]{1,0:T(8,128)(2,1)S(1)}, bf16[296,256]{1,0:T(8,128)(2,1)S(1)}, u32[]{:S(2)}, u32[]{:S(2)}) collective-permute-start(bf16[296,256]{1,0:T(8,128)(2,1)S(1)} %pad_maximum_fusion.3), channel_id=1, source_target_pairs={{16,0},{32,16},{48,32},{64,48},{80,64},{96,80},{112,96},{128,112},... | collective-permute-start | bytes 454664 | tf_op jit(solution)/shard_map/ppermute | solution.py:155
  13.2 8.3 %copy-start.2 = (bf16[296,256]{1,0:T(8,128)(2,1)}, bf16[296,256]{1,0:T(8,128)(2,1)S(1)}, u32[]{:S(2)}) copy-start(bf16[296,256]{1,0:T(8,128)(2,1)S(1)} %collective-permute-done.north_ref) | copy-start | bytes 454660
  17.4 4.1 %copy-start.3 = (bf16[296,256]{1,0:T(8,128)(2,1)}, bf16[296,256]{1,0:T(8,128)(2,1)S(1)}, u32[]{:S(2)}) copy-start(bf16[296,256]{1,0:T(8,128)(2,1)S(1)} %collective-permute-done.1.south_ref) | copy-start | bytes 454660
  17.4 12.3 %collective-permute-start.4 = (bf16[18,24,256]{2,1,0:T(8,128)(2,1)S(1)}, bf16[18,24,256]{2,1,0:T(8,128)(2,1)S(1)}, u32[]{:S(2)}, u32[]{:S(2)}) collective-permute-start(bf16[18,24,256]{2,1,0:T(8,128)(2,1)S(1)} %pad_maximum_fusion), channel_id=1, source_target_pairs={{0,1},{1,2},{2,3},{3,4},{4,5},{5,6},{6,7},{7,8},{8,9},{9,10},{10,1... | collective-permute-start | bytes 663560 | tf_op jit(solution)/shard_map/ppermute | solution.py:155
  17.6 12.2 %collective-permute-start.5 = (bf16[18,24,256]{2,1,0:T(8,128)(2,1)S(1)}, bf16[18,24,256]{2,1,0:T(8,128)(2,1)S(1)}, u32[]{:S(2)}, u32[]{:S(2)}) collective-permute-start(bf16[18,24,256]{2,1,0:T(8,128)(2,1)S(1)} %pad_maximum_fusion.1), channel_id=1, source_target_pairs={{0,15},{1,0},{2,1},{3,2},{4,3},{5,4},{6,5},{7,6},{8,7},{9,8},{10,9... | collective-permute-start | bytes 663560 | tf_op jit(solution)/shard_map/ppermute | solution.py:155
  29.8 0.7 copy-start.5
  29.8 0.8 copy-start.6
  37.4 2.1 %collective-permute-start.6 = (bf16[1024,256]{1,0:T(8,128)(2,1)}, bf16[1024,256]{1,0:T(8,128)(2,1)S(1)}, u32[]{:S(2)}, u32[]{:S(2)}) collective-permute-start(bf16[1024,256]{1,0:T(8,128)(2,1)} %get-tuple-element.14), channel_id=1, source_target_pairs={{0,1},{1,0},{2,3},{3,2},{4,5},{5,4},{6,7},{7,6},{8,9},{9,8},{10,11... | collective-permute-start | bytes 1572872 | tf_op jit(solution)/shard_map/ppermute | solution.py:171
  39.5 13.0 %copy-start.8 = (bf16[34,24,256]{2,1,0:T(8,128)(2,1)S(1)}, bf16[34,24,256]{2,1,0:T(8,128)(2,1)}, u32[]{:S(2)}) copy-start(bf16[34,24,256]{2,1,0:T(8,128)(2,1)} %get-tuple-element.10) | copy-start | bytes 1253380
  39.5 13.0 %copy-start.7 = (bf16[34,24,256]{2,1,0:T(8,128)(2,1)S(1)}, bf16[34,24,256]{2,1,0:T(8,128)(2,1)}, u32[]{:S(2)}) copy-start(bf16[34,24,256]{2,1,0:T(8,128)(2,1)} %get-tuple-element.11) | copy-start | bytes 1253380
  41.0 7.4 %collective-permute-start.7 = (bf16[2,2,2,2,2,8,256]{6,5,4,3,2,1,0:T(8,128)(2,1)S(1)}, bf16[2,2,2,2,2,8,256]{6,5,4,3,2,1,0:T(8,128)(2,1)S(1)}, u32[]{:S(2)}, u32[]{:S(2)}) collective-permute-start(bf16[2,2,2,2,2,8,256]{6,5,4,3,2,1,0:T(8,128)(2,1)S(1)} %get-tuple-element.15), channel_id=1, source_target_pairs={{0,6},{1,7},{2,4},{3,5},{4,2},{5,3},{6,0},{7,1},{8,14},{9,15},{10,... | collective-permute-start | bytes 393224 | tf_op jit(solution)/shard_map/ppermute | solution.py:171
  42.0 6.9 %collective-permute-start.9 = (bf16[2,2,2,2,2,8,256]{6,5,4,3,2,1,0:T(8,128)(2,1)S(1)}, bf16[2,2,2,2,2,8,256]{6,5,4,3,2,1,0:T(8,128)(2,1)S(1)}, u32[]{:S(2)}, u32[]{:S(2)}) collective-permute-start(bf16[2,2,2,2,2,8,256]{6,5,4,3,2,1,0:T(8,128)(2,1)S(1)} %get-tuple-element.16), channel_id=1, source_target_pairs={{0,4},{1,5},{2,6},{3,7},{4,0},{5,1},{6,2},{7,3},{8,12},{9,13},{10,... | collective-permute-start | bytes 393224 | tf_op jit(solution)/shard_map/ppermute | solution.py:171
  42.6 7.7 %collective-permute-start.8 = (bf16[2,2,2,2,2,8,256]{6,5,4,3,2,1,0:T(8,128)(2,1)S(1)}, bf16[2,2,2,2,2,8,256]{6,5,4,3,2,1,0:T(8,128)(2,1)S(1)}, u32[]{:S(2)}, u32[]{:S(2)}) collective-permute-start(bf16[2,2,2,2,2,8,256]{6,5,4,3,2,1,0:T(8,128)(2,1)S(1)} %get-tuple-element.17), channel_id=1, source_target_pairs={{0,2},{1,3},{2,0},{3,1},{4,6},{5,7},{6,4},{7,5},{8,10},{9,11},{10,... | collective-permute-start | bytes 393224 | tf_op jit(solution)/shard_map/ppermute | solution.py:171
  50.4 6.0 %collective-permute-start.10 = (bf16[2,2,2,2,8,256]{5,4,3,2,1,0:T(8,128)(2,1)S(1)}, bf16[2,2,2,2,8,256]{5,4,3,2,1,0:T(8,128)(2,1)S(1)}, u32[]{:S(2)}, u32[]{:S(2)}) collective-permute-start(bf16[2,2,2,2,8,256]{5,4,3,2,1,0:T(8,128)(2,1)S(1)} %fusion.5), channel_id=1, source_target_pairs={{0,8},{1,9},{2,10},{3,11},{4,12},{5,13},{6,14},{7,15},{8,0},{9,1},... | collective-permute-start | bytes 196616 | tf_op jit(solution)/shard_map/ppermute | solution.py:171
  52.5 15.9 %collective-permute-start.2 = (bf16[34,24,256]{2,1,0:T(8,128)(2,1)S(1)}, bf16[34,24,256]{2,1,0:T(8,128)(2,1)S(1)}, u32[]{:S(2)}, u32[]{:S(2)}) collective-permute-start(bf16[34,24,256]{2,1,0:T(8,128)(2,1)S(1)} %copy-done.8), channel_id=1, source_target_pairs={{0,1},{1,2},{2,3},{3,4},{4,5},{5,6},{6,7},{7,8},{8,9},{9,10},{10,1... | collective-permute-start | bytes 1253384 | tf_op jit(solution)/shard_map/ppermute | solution.py:155
  52.5 15.9 %collective-permute-start.3 = (bf16[34,24,256]{2,1,0:T(8,128)(2,1)S(1)}, bf16[34,24,256]{2,1,0:T(8,128)(2,1)S(1)}, u32[]{:S(2)}, u32[]{:S(2)}) collective-permute-start(bf16[34,24,256]{2,1,0:T(8,128)(2,1)S(1)} %copy-done.7), channel_id=1, source_target_pairs={{0,15},{1,0},{2,1},{3,2},{4,3},{5,4},{6,5},{7,6},{8,7},{9,8},{10,9... | collective-permute-start | bytes 1253384 | tf_op jit(solution)/shard_map/ppermute | solution.py:155
  57.1 22.2 %all-to-all-start = ((f32[16,8,256]{2,1,0:T(8,128)}), f32[16,8,256]{2,1,0:T(8,128)S(1)}, u32[]{:S(2)}, u32[]{:S(2)}) async-start(f32[16,8,256]{2,1,0:T(8,128)} %bitcast.23), calls=%async_computation | async-start | bytes 262144 | tf_op jit(solution)/shard_map/all_to_all | solution.py:203
  68.4 0.8 copy-start
  69.2 0.8 copy-start.1
